TPU v7x, 128 devices: a whole 4x4x4 slice. The times are simulated.
128 devices in a mesh: grp: 4 (over y), vir: 32 (over x, z, core).
Axes of the slice: x: 4, y: 4, z: 4, core: 2. Of those that a mesh axis runs over, the one named last changes fastest.
Arguments:
- triplets: int32 [24, 3], P('grp'), may hold values from 0 to 4, as said below
- counts: int32 [4], P('grp'), may hold values from 1 to 6, as said below
- weights: int32 [24], P('grp'), may hold values from 1 to 3
- a_pick: int32 [64], P('vir'), may hold values from 0 to 895, as said below
- occ_energy: float32 [5], replicated, may hold values from -2 to -0.5
- vir_energy: float32 [896], replicated, may hold values from 0.3 to 3
- ints_vvvo: bfloat16 [5, 64, 896, 896], P(None, 'vir'), may hold values from -0.1875 to 0.1875
- t2pair: bfloat16 [5, 5, 896, 896], P(None, None, 'vir'), may hold values from -6 to 6
- t2hole: bfloat16 [5, 60, 64, 896], P(None, None, 'vir'), may hold values from -6 to 6
- ints_hole: bfloat16 [5, 5, 60, 896], replicated, may hold values from -0.75 to 0.75
Outputs:
- trip_energy: float32 [24], P('grp')
- orbital_energy: float32 [64], P('vir')
Inputs may be any that keep to these rules, and one draw needn't show every extreme that they name: `triplets`: each row holds occupied indices i <= j <= k. `counts`: some group has all 6 slots live. `a_pick`: the entries are distinct.
All inputs are finite; a program needn't handle non-finite values.
Results may differ from a plain program's by a relative error of at most 0.0003.
Values may be sent and summed in bfloat16 or wider, within the bound.
A program may use at most 64 MiB of HBM per device.

v0:
```python
import jax
import jax.numpy as jnp
from jax import lax
from jax.experimental import pallas as pl
from jax.experimental.pallas import tpu as pltpu
from jax.sharding import PartitionSpec as P

V = 896
BLOCK = 28
ROWS = 32
PAIRS = 15
OW = 5
LEAD = 2
CHUNK = 224
NT_DIMS = (((1,), (1,)), ((), ()))


def pair_of(step):
    q = PAIRS - 1 - step
    k = (
        (q >= 1).astype(jnp.int32)
        + (q >= 3).astype(jnp.int32)
        + (q >= 6).astype(jnp.int32)
        + (q >= 10).astype(jnp.int32)
    )
    return q, q - k * (k + 1) // 2, k


def kernel(
    t2_ref, vvvo_ref, th_ref, ih_ref, yc_ref, xb_ref, occ_ref, e_ref,
    src, slab, vv, wbuf, send1, recv1, send2, recv2, send3, recv3, vsem,
):
    y = lax.axis_index("grp")
    vir = lax.axis_index("vir")
    core = vir % 2
    x = vir // 8
    z = (vir // 2) % 4

    def place(p):
        is_a = (p % 2) == 0
        u = jnp.where(is_a, x, z)
        w = jnp.where(is_a, z, x)
        off = (y + p // 2) % 4
        return is_a, u, w, off

    def device(is_a, u, w):
        return {"vir": jnp.where(is_a, u * 8 + w * 2, w * 8 + u * 2) + core}

    def first(p):
        is_a, u, w, off = place(p)
        return pltpu.make_async_remote_copy(
            src_ref=src.at[p],
            dst_ref=slab.at[p, core, w],
            send_sem=send1.at[p],
            recv_sem=recv1.at[p],
            device_id=device(is_a, (u + 4 - off) % 4, w),
            device_id_type=pl.DeviceIdType.MESH,
        ), off

    def second(p, turn):
        is_a, u, w, off = place(p)
        shift = (1, 3, 2)[turn]
        return pltpu.make_async_remote_copy(
            src_ref=slab.at[p, core, w],
            dst_ref=slab.at[p, core, w],
            send_sem=send2.at[p, turn],
            recv_sem=recv2.at[p, turn],
            device_id=device(is_a, u, (w + shift) % 4),
            device_id_type=pl.DeviceIdType.MESH,
        )

    def third(p):
        return pltpu.make_async_remote_copy(
            src_ref=slab.at[p, core],
            dst_ref=slab.at[p, core],
            send_sem=send3.at[p],
            recv_sem=recv3.at[p],
            device_id={"vir": vir + 1 - 2 * core},
            device_id_type=pl.DeviceIdType.MESH,
        )

    def load(k):
        return pltpu.make_async_copy(vvvo_ref.at[k], vv.at[k], vsem.at[k])

    barrier = pltpu.get_barrier_semaphore()
    for shift in (1, 2, 3):
        pl.semaphore_signal(
            barrier, inc=1, device_id={"vir": (((x + shift) % 4) * 4 + z) * 2 + core},
            device_id_type=pl.DeviceIdType.MESH)
        pl.semaphore_signal(
            barrier, inc=1, device_id={"vir": (x * 4 + (z + shift) % 4) * 2 + core},
            device_id_type=pl.DeviceIdType.MESH)
    pl.semaphore_signal(
        barrier, inc=1, device_id={"vir": vir + 1 - 2 * core},
        device_id_type=pl.DeviceIdType.MESH)

    for k in range(OW - 1, -1, -1):
        load(k).start()

    def fill(p, carry):
        q, j, k = pair_of(p)
        is_a, u, w, off = place(p)
        block = t2_ref[j, k]
        src[p, BLOCK - 12:, :] = jnp.zeros((ROWS - BLOCK + 12, V), jnp.bfloat16)
        src[p, :BLOCK, :] = block

        @pl.when(off == 0)
        def _():
            slab[p, core, w, BLOCK - 12:, :] = jnp.zeros((ROWS - BLOCK + 12, V), jnp.bfloat16)
            slab[p, core, w, :BLOCK, :] = block

        return carry

    lax.fori_loop(0, PAIRS, fill, 0)
    e_ref[...] = jnp.zeros_like(e_ref)
    pl.semaphore_wait(barrier, 7)

    def start_first(p):
        copy, off = first(p)

        @pl.when(off != 0)
        def _():
            copy.start()

    for p in range(LEAD):
        start_first(p)

    def compute(p):
        q, j, k = pair_of(p)
        is_a, u, w, off = place(p)
        fresh = (p == 0) | (q == (k + 1) * (k + 2) // 2 - 1)

        @pl.when(fresh)
        def _():
            load(k).wait()

        cols = slab[p].reshape(2 * 4 * ROWS, V)
        wbuf[...] = lax.dot_general(vv[k], cols, NT_DIMS, preferred_element_type=jnp.float32)

        row = lax.broadcasted_iota(jnp.int32, (256, 1), 0)
        r_core = row // 128
        r_w = (row // ROWS) % 4
        r_in = row % ROWS
        source = (u + off) % 4
        owner = jnp.where(is_a, source * 8 + r_w * 2, r_w * 8 + source * 2) + r_core
        target = jnp.where(r_in < BLOCK, owner * BLOCK + r_in, -1)
        column = lax.broadcasted_iota(jnp.int32, (256, V), 1)
        select = (column == target).astype(jnp.float32).astype(jnp.bfloat16)
        holes = lax.dot_general(
            select, ih_ref[k, j], NT_DIMS, preferred_element_type=jnp.float32
        ).astype(jnp.bfloat16)
        variant = jnp.where(is_a, 0, 4) + source
        yc_row = yc_ref[pl.ds(variant, 1), :]

        def one(i, carry):
            shift = occ_ref[i] + occ_ref[j] + occ_ref[k]
            yc = yc_row - shift
            for a in range(2):
                total = jnp.zeros((8, 256), jnp.float32)
                for c in range(V // CHUNK):
                    at = a * V + c * CHUNK
                    hole = lax.dot_general(
                        th_ref[i, at:at + CHUNK, :], holes, NT_DIMS,
                        preferred_element_type=jnp.float32)
                    amp = wbuf[at:at + CHUNK, :] + hole
                    base = xb_ref[at:at + CHUNK, :]
                    den = jnp.concatenate([base, base], axis=1) + yc
                    term = amp * amp / den
                    total = total + jnp.sum(term.reshape(CHUNK // 8, 8, 256), axis=0)
                line = jnp.sum(total, axis=0, keepdims=True)
                line = line[:, :128] + line[:, 128:]
                e_ref[pl.ds((q * OW + i) * 2 + a, 1), :] = line
            return carry

        lax.fori_loop(0, j + 1, one, 0)

    def step(s, carry):
        @pl.when(s + LEAD < PAIRS)
        def _():
            start_first(s + LEAD)

        @pl.when(s < PAIRS)
        def _():
            copy, off = first(s)

            @pl.when(off != 0)
            def _():
                copy.wait_recv()

            for turn in range(3):
                second(s, turn).start()

        @pl.when((s >= 1) & (s < PAIRS + 1))
        def _():
            for turn in range(3):
                second(s - 1, turn).wait_recv()
            third(s - 1).start()

        @pl.when(s >= 2)
        def _():
            third(s - 2).wait_recv()
            compute(s - 2)

        return carry

    lax.fori_loop(0, PAIRS + 2, step, 0)

    def drain(p, carry):
        copy, off = first(p)

        @pl.when(off != 0)
        def _():
            copy.wait_send()

        for turn in range(3):
            second(p, turn).wait_send()
        third(p).wait_send()
        return carry

    lax.fori_loop(0, PAIRS, drain, 0)


def from_everyone(value, axis):
    length = lax.axis_size(axis)
    return lax.all_to_all(
        jnp.broadcast_to(value[None], (length, *value.shape)), axis, 0, 0, tiled=True
    )


def over_copies(value, axis):
    return jnp.sum(from_everyone(value, axis), axis=0)


def pick_energy(a_pick, vir_energy):
    columns = jnp.arange(vir_energy.shape[0], dtype=jnp.int32)
    return jnp.sum(jnp.where(a_pick[:, None] == columns[None, :], vir_energy[None, :], 0.0), axis=1)


def tables(a_pick, vir_energy, t2hole):
    e_a = pick_energy(a_pick, vir_energy)
    base = (e_a[:, None] + vir_energy[None, :]).reshape(2 * V, 1)
    xb = jnp.broadcast_to(base, (2 * V, 128))
    split = vir_energy.reshape(4, 4, 2, BLOCK)
    split = jnp.pad(split, ((0, 0), (0, 0), (0, 0), (0, ROWS - BLOCK)), constant_values=1.0)
    by_x = jnp.transpose(split, (0, 2, 1, 3)).reshape(4, 256)
    by_z = jnp.transpose(split, (1, 2, 0, 3)).reshape(4, 256)
    yc = jnp.concatenate([by_x, by_z], axis=0)
    th = -jnp.transpose(t2hole, (0, 2, 3, 1)).reshape(OW, 2 * V, 60)
    return xb, yc, th


def partial_energies(t2pair, ints_vvvo, th, ints_hole, yc, xb, occ_energy):
    vmem = pl.BlockSpec(memory_space=pltpu.VMEM)
    return pl.pallas_call(
        kernel,
        out_shape=jax.ShapeDtypeStruct((160, 128), jnp.float32),
        in_specs=[
            vmem, pl.BlockSpec(memory_space=pl.ANY), vmem, vmem, vmem, vmem,
            pl.BlockSpec(memory_space=pltpu.SMEM),
        ],
        out_specs=vmem,
        scratch_shapes=[
            pltpu.VMEM((PAIRS, ROWS, V), jnp.bfloat16),
            pltpu.VMEM((PAIRS, 2, 4, ROWS, V), jnp.bfloat16),
            pltpu.VMEM((OW, 2 * V, V), jnp.bfloat16),
            pltpu.VMEM((2 * V, 256), jnp.float32),
            pltpu.SemaphoreType.DMA((PAIRS,)),
            pltpu.SemaphoreType.DMA((PAIRS,)),
            pltpu.SemaphoreType.DMA((PAIRS, 3)),
            pltpu.SemaphoreType.DMA((PAIRS, 3)),
            pltpu.SemaphoreType.DMA((PAIRS,)),
            pltpu.SemaphoreType.DMA((PAIRS,)),
            pltpu.SemaphoreType.DMA((OW,)),
        ],
        compiler_params=pltpu.CompilerParams(
            collective_id=0, has_side_effects=True, vmem_limit_bytes=60 * 1024 * 1024
        ),
    )(t2pair, ints_vvvo.reshape(OW, 2 * V, V), th, ints_hole, yc, xb, occ_energy)


def shards(
    triplets, counts, weights, a_pick, occ_energy, vir_energy, ints_vvvo, t2pair, t2hole, ints_hole
):
    slots = triplets.shape[0]
    window = a_pick.shape[0] * lax.axis_size("vir")
    xb, yc, th = tables(a_pick, vir_energy, t2hole)
    lines = partial_energies(t2pair, ints_vvvo, th, ints_hole, yc, xb, occ_energy)
    cells = PAIRS * OW
    energy = jnp.sum(lines[: cells * 2], axis=1)

    code = (triplets[:, 2] * (triplets[:, 2] + 1) // 2 + triplets[:, 1]) * OW + triplets[:, 0]
    live = jnp.arange(slots, dtype=jnp.int32) < counts[0]
    factor = jnp.where(live, -weights.astype(jnp.float32) / (V * V), 0.0)
    hit = jnp.where(code[:, None] == jnp.arange(cells, dtype=jnp.int32)[None, :], factor[:, None], 0.0)
    total = over_copies(jnp.concatenate([energy, jnp.sum(hit, axis=0)]), "grp")
    whole = total[: cells * 2].reshape(cells, 2)
    orbital = jnp.sum(total[cells * 2 :, None] * whole, axis=0)
    mine = jnp.sum(hit * jnp.sum(whole, axis=1)[None, :], axis=1)
    trip_energy = over_copies(mine, "vir") / window
    return (trip_energy, orbital)


def solution(mesh):
    placed = (
        P("grp", None),
        P("grp"),
        P("grp"),
        P("vir"),
        P(),
        P(),
        P(None, "vir", None, None),
        P(None, None, "vir", None),
        P(None, None, "vir", None),
        P(),
    )
    return jax.shard_map(
        shards, mesh=mesh, in_specs=placed, out_specs=(P("grp"), P("vir")), check_vma=False
    )
```

profile of v0, /device:TPU:1, one launch (start us, length us, event | category | flops | bytes accessed | tf_op | source)
XLA Modules:
  0.0 108.1 jit_solution(10643728751609812680)
XLA Ops:
  1.3 0.8 add_bitcast_fusion
  2.1 2.1 %negate_bitcast_fusion = bf16[5,2,896,60]{2,1,3,0:T(2,128)(2,1)S(1)} fusion(bf16[5,60,2,896]{3,2,1,0:T(2,128)(2,1)} %param.18), kind=kLoop, calls=%fused_computation | loop fusion | flops 537600 | bytes 2150400 | tf_op jit(solution)/shard_map/neg | solution.py:248
  4.2 0.0 copy-start
  4.2 0.0 copy-start.1
  4.2 3.2 %copy.25 = bf16[5,2,896,60]{3,2,1,0:T(8,128)(2,1)} copy(bf16[5,2,896,60]{2,1,3,0:T(2,128)(2,1)S(1)} %negate_bitcast_fusion) | data formatting | bytes 2150400 | tf_op jit(solution)/shard_map/neg | solution.py:248
  7.4 0.0 copy-done
  7.4 0.1 reshape.55
  7.6 0.1 reshape.57
  7.7 0.1 reshape.56
  7.8 0.0 copy-done.1
  7.8 0.2 fusion
  7.9 0.1 broadcast_add_fusion
  8.0 0.6 pad_maximum_fusion.yc_ref
  8.6 1.3 %broadcast_in_dim.60.xb_ref = f32[1792,128]{1,0:T(8,128)} broadcast(f32[1792]{0:T(1024)S(1)} %add.39), dimensions={0} | broadcast | bytes 924672 | tf_op jit(solution)/shard_map/broadcast_in_dim | solution.py:242
  9.9 0.0 copy-start.2
  9.9 71.3 %shard_map.113 = f32[160,128]{1,0:T(8,128)} custom-call(bf16[5,5,28,896]{3,2,1,0:T(8,128)(2,1)} %t2_ref.1, bf16[5,1792,896]{2,1,0:T(8,128)(2,1)} %bitcast.13, bf16[5,1792,60]{2,1,0:T(8,128)(2,1)} %bitcast.14, bf16[5,5,60,896]{3,2,1,0:T(8,128)(2,1)} %ih_ref.1, f32[8,256]{1,0:T(8,128)} %pad_maximum_fusion.yc_ref, f32[1792,128]{1,0:T(8,128)} %broadcast_in_dim.60.xb_ref, ...), custom_call_target="tpu_custom_call" | custom-call | tf_op jit(solution)/shard_map/pallas_call | solution.py:254
  81.2 1.0 slice_reduce_fusion
  82.2 0.0 copy-done.2
  82.2 0.1 select_reduce_fusion
  82.3 0.1 pad_maximum_fusion.1
  82.4 10.9 %all_to_all.12 = f32[4,1,225]{2,1,0:T(1,128)S(1)} all-to-all(f32[4,1,225]{2,1,0:T(1,128)S(1)} %broadcast_in_dim.61), channel_id=1, replica_groups=mesh['grp'=4,'vir'=32] {'grp'}, dimensions={0} | all-to-all | bytes 7200 | tf_op jit(solution)/shard_map/all_to_all | solution.py:225
  93.3 0.1 slice.24
  93.3 0.1 reshape.58
  93.5 0.6 multiply_reduce_fusion
  94.1 0.2 fusion.1
  94.3 13.2 %all_to_all.13 = f32[32,1,6]{2,1,0:T(1,128)S(1)} all-to-all(f32[32,1,6]{2,1,0:T(1,128)S(1)} %broadcast_in_dim.62), channel_id=1, replica_groups=mesh['grp'=4,'vir'=32] {'vir'}, dimensions={0} | all-to-all | bytes 1536 | tf_op jit(solution)/shard_map/all_to_all | solution.py:225
  107.5 0.1 reduce_sum.78
  107.5 0.5 broadcast_multiply_fusion
  (8 shorter events, 0.1 us)
Async XLA Ops:
  4.2 3.2 %copy-start = (f32[896]{0:T(1024)S(1)}, f32[896]{0:T(1024)}, u32[]{:S(2)}) copy-start(f32[896]{0:T(1024)} %param.15) | copy-start | bytes 10756
  4.2 3.6 %copy-start.1 = (s32[2]{0:T(128)S(1)}, s32[2]{0:T(128)}, u32[]{:S(2)}) copy-start(s32[2]{0:T(128)} %param.13) | copy-start | bytes 28
  9.9 72.3 %copy-start.2 = (s32[6]{0:T(128)S(1)}, s32[6]{0:T(128)}, u32[]{:S(2)}) copy-start(s32[6]{0:T(128)} %param.12) | copy-start | bytes 76
where the time goes:
time: 108 us
  Pallas kernels  71.3 us (66%)
  blocking collectives  24.1 us (22%)
  other arithmetic  6.33 us (6%)
  local copies, waits for them, and re-layouts  5.03 us (5%)
  between operations  1.36 us (1%)
    pallas_call x1, Pallas kernels, partial_energies(): pl.pallas_call(kernel, out_shape=jax.ShapeDtypeStruct((160, 128), jnp.flo...  71.3 us
    all_to_all x2, blocking collectives, from_everyone(): lax.all_to_all(jnp.broadcast_to(value[None], (length, *value.shape)), axi...  24.1 us
    neg x1, local copies, waits for them, and re-layouts, tables(): th = -jnp.transpose(t2hole, (0, 2, 3, 1)).reshape(OW, 2 * V, 60)  3.2 us

commit v1 on v0

--- a/solution.py
+++ b/solution.py
@@ -10,7 +10,10 @@
 ROWS = 32
 PAIRS = 15
 OW = 5
-LEAD = 2
+LEAD = 4
+LAG2 = 3
+LAG3 = 6
+LAG4 = 8
 CHUNK = 224
 NT_DIMS = (((1,), (1,)), ((), ()))
 
@@ -27,8 +30,9 @@
 
 
 def kernel(
-    t2_ref, vvvo_ref, th_ref, ih_ref, yc_ref, xb_ref, occ_ref, e_ref,
+    t2_ref, vvvo_ref, th_ref, ih_ref, yc_ref, xb_ref, hit_ref, occ_ref, trip_ref, orb_ref,
     src, slab, vv, wbuf, send1, recv1, send2, recv2, send3, recv3, vsem,
+    tile, ybox, part, vbox, ysend, yrecv, psend, precv,
 ):
     y = lax.axis_index("grp")
     vir = lax.axis_index("vir")
@@ -59,7 +63,7 @@
 
     def second(p, turn):
         is_a, u, w, off = place(p)
-        shift = (1, 3, 2)[turn]
+        shift = (1, 3)[turn]
         return pltpu.make_async_remote_copy(
             src_ref=slab.at[p, core, w],
             dst_ref=slab.at[p, core, w],
@@ -69,6 +73,20 @@
             device_id_type=pl.DeviceIdType.MESH,
         )
 
+    def relay(p):
+        is_a, u, w, off = place(p)
+        back = ((p // 2) % 2) == 0
+        slot = jnp.where(back, (w + 1) % 4, (w + 3) % 4)
+        to = jnp.where(back, (w + 3) % 4, (w + 1) % 4)
+        return pltpu.make_async_remote_copy(
+            src_ref=slab.at[p, core, slot],
+            dst_ref=slab.at[p, core, slot],
+            send_sem=send2.at[p, 2],
+            recv_sem=recv2.at[p, 2],
+            device_id=device(is_a, u, to),
+            device_id_type=pl.DeviceIdType.MESH,
+        )
+
     def third(p):
         return pltpu.make_async_remote_copy(
             src_ref=slab.at[p, core],
@@ -83,16 +101,18 @@
         return pltpu.make_async_copy(vvvo_ref.at[k], vv.at[k], vsem.at[k])
 
     barrier = pltpu.get_barrier_semaphore()
-    for shift in (1, 2, 3):
+
+    def greet(r, carry):
         pl.semaphore_signal(
-            barrier, inc=1, device_id={"vir": (((x + shift) % 4) * 4 + z) * 2 + core},
+            barrier, inc=1, device_id={"vir": (vir + r) % 32},
             device_id_type=pl.DeviceIdType.MESH)
+        return carry
+
+    lax.fori_loop(1, 32, greet, 0)
+    for r in (1, 2, 3):
         pl.semaphore_signal(
-            barrier, inc=1, device_id={"vir": (x * 4 + (z + shift) % 4) * 2 + core},
+            barrier, inc=1, device_id={"grp": (y + r) % 4},
             device_id_type=pl.DeviceIdType.MESH)
-    pl.semaphore_signal(
-        barrier, inc=1, device_id={"vir": vir + 1 - 2 * core},
-        device_id_type=pl.DeviceIdType.MESH)
 
     for k in range(OW - 1, -1, -1):
         load(k).start()
@@ -112,8 +132,9 @@
         return carry
 
     lax.fori_loop(0, PAIRS, fill, 0)
-    e_ref[...] = jnp.zeros_like(e_ref)
-    pl.semaphore_wait(barrier, 7)
+    tile[...] = jnp.zeros_like(tile)
+    tile[2:3, :] = jnp.sum(hit_ref[...], axis=0, keepdims=True)
+    pl.semaphore_wait(barrier, 34)
 
     def start_first(p):
         copy, off = first(p)
@@ -151,6 +172,7 @@
         ).astype(jnp.bfloat16)
         variant = jnp.where(is_a, 0, 4) + source
         yc_row = yc_ref[pl.ds(variant, 1), :]
+        lane = lax.broadcasted_iota(jnp.int32, (1, 128), 1)
 
         def one(i, carry):
             shift = occ_ref[i] + occ_ref[j] + occ_ref[k]
@@ -168,8 +190,8 @@
                     term = amp * amp / den
                     total = total + jnp.sum(term.reshape(CHUNK // 8, 8, 256), axis=0)
                 line = jnp.sum(total, axis=0, keepdims=True)
-                line = line[:, :128] + line[:, 128:]
-                e_ref[pl.ds((q * OW + i) * 2 + a, 1), :] = line
+                line = jnp.sum(line, axis=1, keepdims=True)
+                tile[a:a + 1, :] = jnp.where(lane == q * OW + i, line, tile[a:a + 1, :])
             return carry
 
         lax.fori_loop(0, j + 1, one, 0)
@@ -187,23 +209,28 @@
             def _():
                 copy.wait_recv()
 
-            for turn in range(3):
+            for turn in range(2):
                 second(s, turn).start()
 
-        @pl.when((s >= 1) & (s < PAIRS + 1))
-        def _():
-            for turn in range(3):
-                second(s - 1, turn).wait_recv()
-            third(s - 1).start()
-
-        @pl.when(s >= 2)
-        def _():
-            third(s - 2).wait_recv()
-            compute(s - 2)
-
-        return carry
-
-    lax.fori_loop(0, PAIRS + 2, step, 0)
+        @pl.when((s >= LAG2) & (s < PAIRS + LAG2))
+        def _():
+            for turn in range(2):
+                second(s - LAG2, turn).wait_recv()
+            relay(s - LAG2).start()
+
+        @pl.when((s >= LAG3) & (s < PAIRS + LAG3))
+        def _():
+            relay(s - LAG3).wait_recv()
+            third(s - LAG3).start()
+
+        @pl.when(s >= LAG4)
+        def _():
+            third(s - LAG4).wait_recv()
+            compute(s - LAG4)
+
+        return carry
+
+    lax.fori_loop(0, PAIRS + LAG4, step, 0)
 
     def drain(p, carry):
         copy, off = first(p)
@@ -212,23 +239,55 @@
         def _():
             copy.wait_send()
 
-        for turn in range(3):
+        for turn in range(2):
             second(p, turn).wait_send()
+        relay(p).wait_send()
         third(p).wait_send()
         return carry
 
     lax.fori_loop(0, PAIRS, drain, 0)
 
-
-def from_everyone(value, axis):
-    length = lax.axis_size(axis)
-    return lax.all_to_all(
-        jnp.broadcast_to(value[None], (length, *value.shape)), axis, 0, 0, tiled=True
-    )
-
-
-def over_copies(value, axis):
-    return jnp.sum(from_everyone(value, axis), axis=0)
+    def to_group(r):
+        return pltpu.make_async_remote_copy(
+            src_ref=tile,
+            dst_ref=ybox.at[y],
+            send_sem=ysend.at[r - 1],
+            recv_sem=yrecv.at[r - 1],
+            device_id={"grp": (y + r) % 4},
+            device_id_type=pl.DeviceIdType.MESH,
+        )
+
+    for r in (1, 2, 3):
+        to_group(r).start()
+    ybox[y] = tile[...]
+    for r in (1, 2, 3):
+        to_group(r).wait_recv()
+    whole = ybox[0] + ybox[1] + ybox[2] + ybox[3]
+    mine = hit_ref[...] * (whole[0:1, :] + whole[1:2, :])
+    part[...] = mine
+    vbox[vir] = mine
+    orb = jnp.sum(whole[2:3, :] * whole, axis=1, keepdims=True)
+    orb_ref[...] = jnp.broadcast_to(orb, (8, 128))
+
+    def to_plane(r, carry):
+        pltpu.make_async_remote_copy(
+            src_ref=part,
+            dst_ref=vbox.at[vir],
+            send_sem=psend,
+            recv_sem=precv,
+            device_id={"vir": (vir + r) % 32},
+            device_id_type=pl.DeviceIdType.MESH,
+        ).start()
+        return carry
+
+    lax.fori_loop(1, 32, to_plane, 0)
+    for r in (1, 2, 3):
+        to_group(r).wait_send()
+    others = vbox.at[pl.ds(0, 31)]
+    pltpu.make_async_copy(others, others, precv).wait()
+    trip = jnp.sum(jnp.sum(vbox[...], axis=0), axis=1, keepdims=True)
+    trip_ref[...] = jnp.broadcast_to(trip, (8, 128)) / 64
+    pltpu.make_async_copy(others, others, psend).wait()
 
 
 def pick_energy(a_pick, vir_energy):
@@ -249,16 +308,16 @@
     return xb, yc, th
 
 
-def partial_energies(t2pair, ints_vvvo, th, ints_hole, yc, xb, occ_energy):
+def partial_energies(t2pair, ints_vvvo, th, ints_hole, yc, xb, hit, occ_energy):
     vmem = pl.BlockSpec(memory_space=pltpu.VMEM)
     return pl.pallas_call(
         kernel,
-        out_shape=jax.ShapeDtypeStruct((160, 128), jnp.float32),
+        out_shape=[jax.ShapeDtypeStruct((8, 128), jnp.float32)] * 2,
         in_specs=[
-            vmem, pl.BlockSpec(memory_space=pl.ANY), vmem, vmem, vmem, vmem,
+            vmem, pl.BlockSpec(memory_space=pl.ANY), vmem, vmem, vmem, vmem, vmem,
             pl.BlockSpec(memory_space=pltpu.SMEM),
         ],
-        out_specs=vmem,
+        out_specs=[vmem, vmem],
         scratch_shapes=[
             pltpu.VMEM((PAIRS, ROWS, V), jnp.bfloat16),
             pltpu.VMEM((PAIRS, 2, 4, ROWS, V), jnp.bfloat16),
@@ -271,33 +330,34 @@
             pltpu.SemaphoreType.DMA((PAIRS,)),
             pltpu.SemaphoreType.DMA((PAIRS,)),
             pltpu.SemaphoreType.DMA((OW,)),
+            pltpu.VMEM((8, 128), jnp.float32),
+            pltpu.VMEM((4, 8, 128), jnp.float32),
+            pltpu.VMEM((8, 128), jnp.float32),
+            pltpu.VMEM((32, 8, 128), jnp.float32),
+            pltpu.SemaphoreType.DMA((3,)),
+            pltpu.SemaphoreType.DMA((3,)),
+            pltpu.SemaphoreType.DMA,
+            pltpu.SemaphoreType.DMA,
         ],
         compiler_params=pltpu.CompilerParams(
             collective_id=0, has_side_effects=True, vmem_limit_bytes=60 * 1024 * 1024
         ),
-    )(t2pair, ints_vvvo.reshape(OW, 2 * V, V), th, ints_hole, yc, xb, occ_energy)
+    )(t2pair, ints_vvvo.reshape(OW, 2 * V, V), th, ints_hole, yc, xb, hit, occ_energy)
 
 
 def shards(
     triplets, counts, weights, a_pick, occ_energy, vir_energy, ints_vvvo, t2pair, t2hole, ints_hole
 ):
     slots = triplets.shape[0]
-    window = a_pick.shape[0] * lax.axis_size("vir")
     xb, yc, th = tables(a_pick, vir_energy, t2hole)
-    lines = partial_energies(t2pair, ints_vvvo, th, ints_hole, yc, xb, occ_energy)
-    cells = PAIRS * OW
-    energy = jnp.sum(lines[: cells * 2], axis=1)
-
     code = (triplets[:, 2] * (triplets[:, 2] + 1) // 2 + triplets[:, 1]) * OW + triplets[:, 0]
     live = jnp.arange(slots, dtype=jnp.int32) < counts[0]
     factor = jnp.where(live, -weights.astype(jnp.float32) / (V * V), 0.0)
-    hit = jnp.where(code[:, None] == jnp.arange(cells, dtype=jnp.int32)[None, :], factor[:, None], 0.0)
-    total = over_copies(jnp.concatenate([energy, jnp.sum(hit, axis=0)]), "grp")
-    whole = total[: cells * 2].reshape(cells, 2)
-    orbital = jnp.sum(total[cells * 2 :, None] * whole, axis=0)
-    mine = jnp.sum(hit * jnp.sum(whole, axis=1)[None, :], axis=1)
-    trip_energy = over_copies(mine, "vir") / window
-    return (trip_energy, orbital)
+    lanes = jnp.arange(128, dtype=jnp.int32)
+    hit = jnp.where(code[:, None] == lanes[None, :], factor[:, None], 0.0)
+    hit = jnp.pad(hit, ((0, 8 - slots), (0, 0)))
+    trip, orbital = partial_energies(t2pair, ints_vvvo, th, ints_hole, yc, xb, hit, occ_energy)
+    return (trip[:slots, 0], orbital[:2, 0])
 
 
 def solution(mesh):

time: 108 us -> 91.9 us (0.85)
  blocking collectives: 24.1 us -> 0 us
  Pallas kernels: 71.3 us -> 79.2 us
  other arithmetic: 6.33 us -> 3.06 us
  local copies, waits for them, and re-layouts: 5.03 us -> 8 us
    all_to_all x2 -> x0, blocking collectives: 24.1 us -> none  [from_everyone(): lax.all_to_all(jnp.broadcast_to(value[None], (length, *value.shape)), axi...]
    pallas_call x1, Pallas kernels: 71.3 us -> 79.2 us  [partial_energies(): pl.pallas_call(kernel, out_shape=[jax.ShapeDtypeStruct((8, 128), jnp.floa...]
    slice x1 -> x2, local copies, waits for them, and re-layouts: 0.07 us -> 2.6 us  [shards(): return (trip[:slots, 0], orbital[:2, 0])]
    reduce_sum x6 -> x0, other arithmetic: 1.96 us -> none  [the longest x1 1 us: shards(): energy = jnp.sum(lines[:cells * 2], axis=1)]
where the time goes in v1:
time: 91.9 us; the launch traced here: 91.7 us
  Pallas kernels  79.2 us (86%)
  local copies, waits for them, and re-layouts  8 us (9%)
  other arithmetic  3.06 us (3%)
  between operations  1.37 us (1%)
    pallas_call x1, Pallas kernels, partial_energies(): pl.pallas_call(kernel, out_shape=[jax.ShapeDtypeStruct((8, 128), jnp.floa...  79.2 us
    neg x1, local copies, waits for them, and re-layouts, tables(): th = -jnp.transpose(t2hole, (0, 2, 3, 1)).reshape(OW, 2 * V, 60)  3.2 us
    slice x2, local copies, waits for them, and re-layouts, shards(): return (trip[:slots, 0], orbital[:2, 0])  2.6 us
    neg x1, other arithmetic, tables(): th = -jnp.transpose(t2hole, (0, 2, 3, 1)).reshape(OW, 2 * V, 60)  2.1 us

profile of v1, /device:TPU:1, one launch (start us, length us, event | category | flops | bytes accessed | tf_op | source)
XLA Modules:
  0.0 91.7 jit_solution(17546684650695648156)
XLA Ops:
  0.6 2.1 %negate_bitcast_fusion = bf16[5,2,896,60]{2,1,3,0:T(2,128)(2,1)S(1)} fusion(bf16[5,60,2,896]{3,2,1,0:T(2,128)(2,1)} %param.18), kind=kLoop, calls=%fused_computation | loop fusion | flops 537600 | bytes 2150400 | tf_op jit(solution)/shard_map/neg | solution.py:307
  2.7 0.0 copy-start
  2.7 0.0 copy-start.2
  2.8 0.0 copy-start.3
  2.8 0.0 copy-start.1
  2.8 3.2 %copy.17 = bf16[5,2,896,60]{3,2,1,0:T(8,128)(2,1)} copy(bf16[5,2,896,60]{2,1,3,0:T(2,128)(2,1)S(1)} %negate_bitcast_fusion) | data formatting | bytes 2150400 | tf_op jit(solution)/shard_map/neg | solution.py:307
  6.0 0.0 copy-done
  6.0 0.1 reshape.38
  6.1 0.1 reshape.40
  6.2 0.1 reshape.39
  6.3 0.6 pad_maximum_fusion.yc_ref
  6.9 0.0 copy-done.2
  6.9 0.2 fusion
  7.1 0.1 broadcast_add_fusion
  7.2 1.3 %broadcast_in_dim.43.xb_ref = f32[1792,128]{1,0:T(8,128)} broadcast(f32[1792]{0:T(1024)S(1)} %add.38), dimensions={0} | broadcast | bytes 924672 | tf_op jit(solution)/shard_map/broadcast_in_dim | solution.py:301
  9.1 0.0 copy-done.3
  9.1 0.0 copy-done.1
  9.2 0.1 fusion.1
  9.2 0.6 pad.9.hit_ref
  9.8 79.2 %shard_map.113 = (f32[8,128]{1,0:T(8,128)}, f32[8,128]{1,0:T(8,128)}) custom-call(bf16[5,5,28,896]{3,2,1,0:T(8,128)(2,1)} %t2_ref.1, bf16[5,1792,896]{2,1,0:T(8,128)(2,1)} %bitcast.12, bf16[5,1792,60]{2,1,0:T(8,128)(2,1)} %bitcast.13, bf16[5,5,60,896]{3,2,1,0:T(8,128)(2,1)} %ih_ref.1, f32[8,256]{1,0:T(8,128)} %pad_maximum_fusion.yc_ref, ...), custom_call_target="tpu_custom_call" | custom-call | tf_op jit(solution)/shard_map/pallas_call | solution.py:313
  89.1 1.3 %slice_reduce_fusion = f32[6]{0:T(128)} fusion(f32[8,128]{1,0:T(8,128)} %get-tuple-element.4), kind=kLoop, calls=%fused_computation.6 | loop fusion | bytes 48 | tf_op jit(solution)/shard_map/slice | solution.py:360
  90.4 1.3 %slice_reduce_fusion.1 = f32[2]{0:T(128)} fusion(f32[8,128]{1,0:T(8,128)} %get-tuple-element.5), kind=kLoop, calls=%fused_computation.15 | loop fusion | bytes 16 | tf_op jit(solution)/shard_map/slice | solution.py:360
  (6 shorter events, 0.1 us)
Async XLA Ops:
  2.7 3.3 %copy-start = (f32[896]{0:T(1024)S(1)}, f32[896]{0:T(1024)}, u32[]{:S(2)}) copy-start(f32[896]{0:T(1024)} %param.15) | copy-start | bytes 10756
  2.7 4.2 %copy-start.2 = (s32[2]{0:T(128)S(1)}, s32[2]{0:T(128)}, u32[]{:S(2)}) copy-start(s32[2]{0:T(128)} %param.13) | copy-start | bytes 28
  2.8 6.4 %copy-start.3 = (s32[6]{0:T(128)S(1)}, s32[6]{0:T(128)}, u32[]{:S(2)}) copy-start(s32[6]{0:T(128)} %param.12) | copy-start | bytes 76
  2.8 6.4 %copy-start.1 = (s32[6,3]{0,1:T(4,128)S(1)}, s32[6,3]{0,1:T(4,128)}, u32[]{:S(2)}) copy-start(s32[6,3]{0,1:T(4,128)} %param.10) | copy-start | bytes 220

commit v2 on v1

--- a/solution.py
+++ b/solution.py
@@ -30,8 +30,8 @@
 
 
 def kernel(
-    t2_ref, vvvo_ref, th_ref, ih_ref, yc_ref, xb_ref, hit_ref, occ_ref, trip_ref, orb_ref,
-    src, slab, vv, wbuf, send1, recv1, send2, recv2, send3, recv3, vsem,
+    t2_ref, vvvo_ref, hole_hbm, ih_hbm, vir_ref, yc_ref, hit_ref, occ_ref, vsm_ref, pick_ref,
+    trip_ref, orb_ref, src, slab, vv, wbuf, th_ref, hole_ref, ih_ref, xb_ref, isem, send1, recv1, send2, recv2, send3, recv3, vsem,
     tile, ybox, part, vbox, ysend, yrecv, psend, precv,
 ):
     y = lax.axis_index("grp")
@@ -54,7 +54,7 @@
         is_a, u, w, off = place(p)
         return pltpu.make_async_remote_copy(
             src_ref=src.at[p],
-            dst_ref=slab.at[p, core, w],
+            dst_ref=slab.at[p, core, w, :, pl.ds(0, V)],
             send_sem=send1.at[p],
             recv_sem=recv1.at[p],
             device_id=device(is_a, (u + 4 - off) % 4, w),
@@ -65,8 +65,8 @@
         is_a, u, w, off = place(p)
         shift = (1, 3)[turn]
         return pltpu.make_async_remote_copy(
-            src_ref=slab.at[p, core, w],
-            dst_ref=slab.at[p, core, w],
+            src_ref=slab.at[p, core, w, :, pl.ds(0, V)],
+            dst_ref=slab.at[p, core, w, :, pl.ds(0, V)],
             send_sem=send2.at[p, turn],
             recv_sem=recv2.at[p, turn],
             device_id=device(is_a, u, (w + shift) % 4),
@@ -79,8 +79,8 @@
         slot = jnp.where(back, (w + 1) % 4, (w + 3) % 4)
         to = jnp.where(back, (w + 3) % 4, (w + 1) % 4)
         return pltpu.make_async_remote_copy(
-            src_ref=slab.at[p, core, slot],
-            dst_ref=slab.at[p, core, slot],
+            src_ref=slab.at[p, core, slot, :, pl.ds(0, V)],
+            dst_ref=slab.at[p, core, slot, :, pl.ds(0, V)],
             send_sem=send2.at[p, 2],
             recv_sem=recv2.at[p, 2],
             device_id=device(is_a, u, to),
@@ -89,8 +89,8 @@
 
     def third(p):
         return pltpu.make_async_remote_copy(
-            src_ref=slab.at[p, core],
-            dst_ref=slab.at[p, core],
+            src_ref=slab.at[p, core, :, :, pl.ds(0, V)],
+            dst_ref=slab.at[p, core, :, :, pl.ds(0, V)],
             send_sem=send3.at[p],
             recv_sem=recv3.at[p],
             device_id={"vir": vir + 1 - 2 * core},
@@ -98,7 +98,7 @@
         )
 
     def load(k):
-        return pltpu.make_async_copy(vvvo_ref.at[k], vv.at[k], vsem.at[k])
+        return pltpu.make_async_copy(vvvo_ref.at[k], vv.at[k, :, pl.ds(0, V)], vsem.at[k])
 
     barrier = pltpu.get_barrier_semaphore()
 
@@ -114,7 +114,12 @@
             barrier, inc=1, device_id={"grp": (y + r) % 4},
             device_id_type=pl.DeviceIdType.MESH)
 
-    for k in range(OW - 1, -1, -1):
+    holes_in = pltpu.make_async_copy(hole_hbm, hole_ref, isem.at[0])
+    ints_in = pltpu.make_async_copy(ih_hbm, ih_ref, isem.at[1])
+    holes_in.start()
+    load(OW - 1).start()
+    ints_in.start()
+    for k in range(OW - 2, -1, -1):
         load(k).start()
 
     def fill(p, carry):
@@ -126,12 +131,17 @@
 
         @pl.when(off == 0)
         def _():
-            slab[p, core, w, BLOCK - 12:, :] = jnp.zeros((ROWS - BLOCK + 12, V), jnp.bfloat16)
-            slab[p, core, w, :BLOCK, :] = block
+            slab[p, core, w, BLOCK - 12:, :V] = jnp.zeros((ROWS - BLOCK + 12, V), jnp.bfloat16)
+            slab[p, core, w, :BLOCK, :V] = block
 
         return carry
 
     lax.fori_loop(0, PAIRS, fill, 0)
+    for a in range(2):
+        e_a = vsm_ref[pick_ref[a]]
+        for c in range(V // 128):
+            lines = jnp.broadcast_to(vir_ref[:, c * 128:(c + 1) * 128], (128, 128))
+            xb_ref[a * V + c * 128:a * V + (c + 1) * 128, :] = lines.T + e_a
     tile[...] = jnp.zeros_like(tile)
     tile[2:3, :] = jnp.sum(hit_ref[...], axis=0, keepdims=True)
     pl.semaphore_wait(barrier, 34)
@@ -145,6 +155,23 @@
 
     for p in range(LEAD):
         start_first(p)
+
+    def turn_holes(i):
+        for c in range(2 * V // 128):
+            at = c * 128
+            base = hole_ref[0, :, at:at + 128].astype(jnp.float32)
+            this = hole_ref[i, :, at:at + 128].astype(jnp.float32)
+            both = jnp.concatenate([base, -this], axis=0)
+            th_ref[i, at:at + 128, :] = both.T.astype(jnp.bfloat16)
+
+    def base_holes():
+        for c in range(2 * V // 128):
+            at = c * 128
+            base = hole_ref[0, :, at:at + 128].astype(jnp.float32)
+            both = jnp.concatenate([-base, jnp.zeros_like(base)], axis=0)
+            turned = both.T.astype(jnp.bfloat16)
+            for k in range(OW):
+                vv[k, at:at + 128, V:] = turned
 
     def compute(p):
         q, j, k = pair_of(p)
@@ -154,9 +181,6 @@
         @pl.when(fresh)
         def _():
             load(k).wait()
-
-        cols = slab[p].reshape(2 * 4 * ROWS, V)
-        wbuf[...] = lax.dot_general(vv[k], cols, NT_DIMS, preferred_element_type=jnp.float32)
 
         row = lax.broadcasted_iota(jnp.int32, (256, 1), 0)
         r_core = row // 128
@@ -169,14 +193,37 @@
         select = (column == target).astype(jnp.float32).astype(jnp.bfloat16)
         holes = lax.dot_general(
             select, ih_ref[k, j], NT_DIMS, preferred_element_type=jnp.float32
-        ).astype(jnp.bfloat16)
+        )
+        blank = jnp.zeros((256, 4), jnp.float32)
+        holes = jnp.concatenate([holes, blank, holes, blank], axis=1).astype(jnp.bfloat16)
+        slab[p, :, :, :, V:] = holes.reshape(2, 4, ROWS, 128)
+        cols = slab[p].reshape(2 * 4 * ROWS, 1024)
+        wbuf[...] = lax.dot_general(vv[k], cols, NT_DIMS, preferred_element_type=jnp.float32)
         variant = jnp.where(is_a, 0, 4) + source
         yc_row = yc_ref[pl.ds(variant, 1), :]
         lane = lax.broadcasted_iota(jnp.int32, (1, 128), 1)
 
+        def terms(amp, at, yc):
+            base = xb_ref[at:at + CHUNK, :]
+            den = jnp.concatenate([base, base], axis=1) + yc
+            term = amp * amp / den
+            return jnp.sum(term.reshape(CHUNK // 8, 8, 256), axis=0)
+
+        def put(total, i, a):
+            line = jnp.sum(total, axis=0, keepdims=True)
+            line = jnp.sum(line, axis=1, keepdims=True)
+            tile[a:a + 1, :] = jnp.where(lane == q * OW + i, line, tile[a:a + 1, :])
+
+        yc = yc_row - (occ_ref[0] + occ_ref[j] + occ_ref[k])
+        for a in range(2):
+            total = jnp.zeros((8, 256), jnp.float32)
+            for c in range(V // CHUNK):
+                at = a * V + c * CHUNK
+                total = total + terms(wbuf[at:at + CHUNK, :], at, yc)
+            put(total, 0, a)
+
         def one(i, carry):
-            shift = occ_ref[i] + occ_ref[j] + occ_ref[k]
-            yc = yc_row - shift
+            yc = yc_row - (occ_ref[i] + occ_ref[j] + occ_ref[k])
             for a in range(2):
                 total = jnp.zeros((8, 256), jnp.float32)
                 for c in range(V // CHUNK):
@@ -184,17 +231,11 @@
                     hole = lax.dot_general(
                         th_ref[i, at:at + CHUNK, :], holes, NT_DIMS,
                         preferred_element_type=jnp.float32)
-                    amp = wbuf[at:at + CHUNK, :] + hole
-                    base = xb_ref[at:at + CHUNK, :]
-                    den = jnp.concatenate([base, base], axis=1) + yc
-                    term = amp * amp / den
-                    total = total + jnp.sum(term.reshape(CHUNK // 8, 8, 256), axis=0)
-                line = jnp.sum(total, axis=0, keepdims=True)
-                line = jnp.sum(line, axis=1, keepdims=True)
-                tile[a:a + 1, :] = jnp.where(lane == q * OW + i, line, tile[a:a + 1, :])
+                    total = total + terms(wbuf[at:at + CHUNK, :] + hole, at, yc)
+                put(total, i, a)
             return carry
 
-        lax.fori_loop(0, j + 1, one, 0)
+        lax.fori_loop(1, j + 1, one, 0)
 
     def step(s, carry):
         @pl.when(s + LEAD < PAIRS)
@@ -222,6 +263,19 @@
         def _():
             relay(s - LAG3).wait_recv()
             third(s - LAG3).start()
+
+        @pl.when(s == 1)
+        def _():
+            holes_in.wait()
+            base_holes()
+
+        @pl.when((s >= 2) & (s < OW + 1))
+        def _():
+            turn_holes(s - 1)
+
+        @pl.when(s == OW + 1)
+        def _():
+            ints_in.wait()
 
         @pl.when(s >= LAG4)
         def _():
@@ -290,39 +344,37 @@
     pltpu.make_async_copy(others, others, psend).wait()
 
 
-def pick_energy(a_pick, vir_energy):
-    columns = jnp.arange(vir_energy.shape[0], dtype=jnp.int32)
-    return jnp.sum(jnp.where(a_pick[:, None] == columns[None, :], vir_energy[None, :], 0.0), axis=1)
-
-
-def tables(a_pick, vir_energy, t2hole):
-    e_a = pick_energy(a_pick, vir_energy)
-    base = (e_a[:, None] + vir_energy[None, :]).reshape(2 * V, 1)
-    xb = jnp.broadcast_to(base, (2 * V, 128))
+def tables(vir_energy, t2hole):
     split = vir_energy.reshape(4, 4, 2, BLOCK)
     split = jnp.pad(split, ((0, 0), (0, 0), (0, 0), (0, ROWS - BLOCK)), constant_values=1.0)
     by_x = jnp.transpose(split, (0, 2, 1, 3)).reshape(4, 256)
     by_z = jnp.transpose(split, (1, 2, 0, 3)).reshape(4, 256)
     yc = jnp.concatenate([by_x, by_z], axis=0)
-    th = -jnp.transpose(t2hole, (0, 2, 3, 1)).reshape(OW, 2 * V, 60)
-    return xb, yc, th
-
-
-def partial_energies(t2pair, ints_vvvo, th, ints_hole, yc, xb, hit, occ_energy):
+    holes = jnp.pad(t2hole.reshape(OW, 60, 2 * V), ((0, 0), (0, 4), (0, 0)))
+    return yc, holes
+
+
+def partial_energies(t2pair, ints_vvvo, holes, ints_hole, vir_energy, yc, hit, occ_energy, a_pick):
     vmem = pl.BlockSpec(memory_space=pltpu.VMEM)
+    smem = pl.BlockSpec(memory_space=pltpu.SMEM)
+    hbm = pl.BlockSpec(memory_space=pl.ANY)
     return pl.pallas_call(
         kernel,
         out_shape=[jax.ShapeDtypeStruct((8, 128), jnp.float32)] * 2,
         in_specs=[
-            vmem, pl.BlockSpec(memory_space=pl.ANY), vmem, vmem, vmem, vmem, vmem,
-            pl.BlockSpec(memory_space=pltpu.SMEM),
+            vmem, hbm, hbm, hbm, vmem, vmem, vmem, smem, smem, smem,
         ],
         out_specs=[vmem, vmem],
         scratch_shapes=[
             pltpu.VMEM((PAIRS, ROWS, V), jnp.bfloat16),
-            pltpu.VMEM((PAIRS, 2, 4, ROWS, V), jnp.bfloat16),
-            pltpu.VMEM((OW, 2 * V, V), jnp.bfloat16),
+            pltpu.VMEM((PAIRS, 2, 4, ROWS, 1024), jnp.bfloat16),
+            pltpu.VMEM((OW, 2 * V, 1024), jnp.bfloat16),
             pltpu.VMEM((2 * V, 256), jnp.float32),
+            pltpu.VMEM((OW, 2 * V, 128), jnp.bfloat16),
+            pltpu.VMEM((OW, 64, 2 * V), jnp.bfloat16),
+            pltpu.VMEM((OW, OW, 60, V), jnp.bfloat16),
+            pltpu.VMEM((2 * V, 128), jnp.float32),
+            pltpu.SemaphoreType.DMA((2,)),
             pltpu.SemaphoreType.DMA((PAIRS,)),
             pltpu.SemaphoreType.DMA((PAIRS,)),
             pltpu.SemaphoreType.DMA((PAIRS, 3)),
@@ -342,21 +394,26 @@
         compiler_params=pltpu.CompilerParams(
             collective_id=0, has_side_effects=True, vmem_limit_bytes=60 * 1024 * 1024
         ),
-    )(t2pair, ints_vvvo.reshape(OW, 2 * V, V), th, ints_hole, yc, xb, hit, occ_energy)
+    )(
+        t2pair, ints_vvvo.reshape(OW, 2 * V, V), holes, ints_hole,
+        vir_energy.reshape(1, V), yc, hit, occ_energy, vir_energy, a_pick,
+    )
 
 
 def shards(
     triplets, counts, weights, a_pick, occ_energy, vir_energy, ints_vvvo, t2pair, t2hole, ints_hole
 ):
     slots = triplets.shape[0]
-    xb, yc, th = tables(a_pick, vir_energy, t2hole)
+    yc, holes = tables(vir_energy, t2hole)
     code = (triplets[:, 2] * (triplets[:, 2] + 1) // 2 + triplets[:, 1]) * OW + triplets[:, 0]
     live = jnp.arange(slots, dtype=jnp.int32) < counts[0]
     factor = jnp.where(live, -weights.astype(jnp.float32) / (V * V), 0.0)
     lanes = jnp.arange(128, dtype=jnp.int32)
     hit = jnp.where(code[:, None] == lanes[None, :], factor[:, None], 0.0)
     hit = jnp.pad(hit, ((0, 8 - slots), (0, 0)))
-    trip, orbital = partial_energies(t2pair, ints_vvvo, th, ints_hole, yc, xb, hit, occ_energy)
+    trip, orbital = partial_energies(
+        t2pair, ints_vvvo, holes, ints_hole, vir_energy, yc, hit, occ_energy, a_pick
+    )
     return (trip[:slots, 0], orbital[:2, 0])
 
 

time: 91.9 us -> 81.6 us (0.89)
  Pallas kernels: 79.2 us -> 71.1 us
  other arithmetic: 3.06 us -> 0.69 us
    pallas_call x1, Pallas kernels: 79.2 us -> 71.1 us  [partial_energies(): pl.pallas_call(kernel, out_shape=[jax.ShapeDtypeStruct((8, 128), jnp.floa...]
    reshape x0 -> x2, local copies, waits for them, and re-layouts: none -> 3.58 us  [the longest x1 2.99 us: tables(): holes = jnp.pad(t2hole.reshape(OW, 60, 2 * V), ((0, 0), (0, 4), (0, 0)))]
    neg x1 -> x0, local copies, waits for them, and re-layouts: 3.2 us -> none  [tables(): th = -jnp.transpose(t2hole, (0, 2, 3, 1)).reshape(OW, 2 * V, 60)]
    neg x1 -> x0, other arithmetic: 2.1 us -> none  [tables(): th = -jnp.transpose(t2hole, (0, 2, 3, 1)).reshape(OW, 2 * V, 60)]
    broadcast_in_dim x1 -> x0, local copies, waits for them, and re-layouts: 1.26 us -> none  [tables(): xb = jnp.broadcast_to(base, (2 * V, 128))]
    pad x0 -> x1, local copies, waits for them, and re-layouts: none -> 1.09 us  [tables(): holes = jnp.pad(t2hole.reshape(OW, 60, 2 * V), ((0, 0), (0, 4), (0, 0)))]
where the time goes in v2:
time: 81.6 us; the launch traced here: 81.3 us
  Pallas kernels  71.1 us (87%)
  local copies, waits for them, and re-layouts  8.2 us (10%)
  between operations  1.37 us (2%)
    pallas_call x1, Pallas kernels, partial_energies(): pl.pallas_call(kernel, out_shape=[jax.ShapeDtypeStruct((8, 128), jnp.floa...  71.1 us
    reshape x1, local copies, waits for them, and re-layouts, tables(): holes = jnp.pad(t2hole.reshape(OW, 60, 2 * V), ((0, 0), (0, 4), (0, 0)))  2.99 us
    slice x2, local copies, waits for them, and re-layouts, shards(): return (trip[:slots, 0], orbital[:2, 0])  2.6 us

profile of v2, /device:TPU:1, one launch (start us, length us, event | category | flops | bytes accessed | tf_op | source)
XLA Modules:
  0.0 81.3 jit_solution(14617765978230572404)
XLA Ops:
  0.6 3.0 %reshape.24 = bf16[5,60,1792]{2,1,0:T(8,128)(2,1)S(1)} reshape(bf16[5,60,2,896]{3,2,1,0:T(2,128)(2,1)} %param.18) | data formatting | bytes 2150400 | tf_op jit(solution)/shard_map/reshape | solution.py:353
  3.6 0.0 copy-start
  3.6 0.0 copy-start.2
  3.6 0.0 copy-start.1
  3.7 1.1 %pad.12.hole_hbm = bf16[5,64,1792]{2,1,0:T(8,128)(2,1)} pad(bf16[5,60,1792]{2,1,0:T(8,128)(2,1)S(1)} %reshape.24, bf16[]{:T(256)} %constant.20.clone.1), padding=0_0x0_4x0_0 | pad | bytes 2222082 | tf_op jit(solution)/shard_map/jit(_pad)/pad | solution.py:353
  4.7 0.0 copy-done
  4.8 0.6 reshape.25.vir_ref
  5.3 0.1 reshape.26
  5.5 0.1 reshape.28
  5.6 0.1 reshape.27
  5.7 0.6 pad_maximum_fusion.yc_ref
  6.9 0.0 copy-done.2
  6.9 0.0 copy-done.1
  7.0 0.1 fusion
  7.1 0.6 pad.14.hit_ref
  7.7 71.1 %shard_map.113 = (f32[8,128]{1,0:T(8,128)}, f32[8,128]{1,0:T(8,128)}) custom-call(bf16[5,5,28,896]{3,2,1,0:T(8,128)(2,1)} %t2_ref.1, bf16[5,1792,896]{2,1,0:T(8,128)(2,1)} %bitcast.9, bf16[5,64,1792]{2,1,0:T(8,128)(2,1)} %pad.12.hole_hbm, bf16[5,5,60,896]{3,2,1,0:T(8,128)(2,1)} %ih_hbm.1, f32[1,896]{1,0:T(1,128)} %reshape.25.vir_ref, ...), custom_call_target="tpu_custom_call" | custom-call | tf_op jit(solution)/shard_map/pallas_call | solution.py:361
  78.7 1.3 %slice_reduce_fusion = f32[6]{0:T(128)} fusion(f32[8,128]{1,0:T(8,128)} %get-tuple-element.4), kind=kLoop, calls=%fused_computation.3 | loop fusion | bytes 48 | tf_op jit(solution)/shard_map/slice | solution.py:417
  80.0 1.3 %slice_reduce_fusion.1 = f32[2]{0:T(128)} fusion(f32[8,128]{1,0:T(8,128)} %get-tuple-element.5), kind=kLoop, calls=%fused_computation.11 | loop fusion | bytes 16 | tf_op jit(solution)/shard_map/slice | solution.py:417
  (5 shorter events, 0.0 us)
Async XLA Ops:
  3.6 1.1 %copy-start = (f32[896]{0:T(1024)S(1)}, f32[896]{0:T(1024)}, u32[]{:S(2)}) copy-start(f32[896]{0:T(1024)} %vsm_ref.1) | copy-start | bytes 10756
  3.6 3.3 %copy-start.2 = (s32[6]{0:T(128)S(1)}, s32[6]{0:T(128)}, u32[]{:S(2)}) copy-start(s32[6]{0:T(128)} %param.12) | copy-start | bytes 76
  3.6 3.3 %copy-start.1 = (s32[6,3]{0,1:T(4,128)S(1)}, s32[6,3]{0,1:T(4,128)}, u32[]{:S(2)}) copy-start(s32[6,3]{0,1:T(4,128)} %param.10) | copy-start | bytes 220

commit v3 on v2

--- a/solution.py
+++ b/solution.py
@@ -12,8 +12,9 @@
 OW = 5
 LEAD = 4
 LAG2 = 3
-LAG3 = 6
-LAG4 = 8
+LAG3 = 3
+LAG4 = 5
+EARLY = 15
 CHUNK = 224
 NT_DIMS = (((1,), (1,)), ((), ()))
 
@@ -63,7 +64,7 @@
 
     def second(p, turn):
         is_a, u, w, off = place(p)
-        shift = (1, 3)[turn]
+        shift = (1, 3, 2)[turn]
         return pltpu.make_async_remote_copy(
             src_ref=slab.at[p, core, w, :, pl.ds(0, V)],
             dst_ref=slab.at[p, core, w, :, pl.ds(0, V)],
@@ -117,8 +118,8 @@
     holes_in = pltpu.make_async_copy(hole_hbm, hole_ref, isem.at[0])
     ints_in = pltpu.make_async_copy(ih_hbm, ih_ref, isem.at[1])
     holes_in.start()
+    ints_in.start()
     load(OW - 1).start()
-    ints_in.start()
     for k in range(OW - 2, -1, -1):
         load(k).start()
 
@@ -156,32 +157,30 @@
     for p in range(LEAD):
         start_first(p)
 
+    def read_holes(i, at):
+        some = hole_ref[i, :, at:at + 128].astype(jnp.float32)
+        return jnp.concatenate([some, jnp.zeros((4, 128), jnp.float32)], axis=0)
+
     def turn_holes(i):
         for c in range(2 * V // 128):
             at = c * 128
-            base = hole_ref[0, :, at:at + 128].astype(jnp.float32)
-            this = hole_ref[i, :, at:at + 128].astype(jnp.float32)
+            base = read_holes(0, at)
+            this = read_holes(i, at)
             both = jnp.concatenate([base, -this], axis=0)
             th_ref[i, at:at + 128, :] = both.T.astype(jnp.bfloat16)
 
     def base_holes():
         for c in range(2 * V // 128):
             at = c * 128
-            base = hole_ref[0, :, at:at + 128].astype(jnp.float32)
+            base = read_holes(0, at)
             both = jnp.concatenate([-base, jnp.zeros_like(base)], axis=0)
             turned = both.T.astype(jnp.bfloat16)
             for k in range(OW):
                 vv[k, at:at + 128, V:] = turned
 
-    def compute(p):
+    def prepare(p, carry):
         q, j, k = pair_of(p)
         is_a, u, w, off = place(p)
-        fresh = (p == 0) | (q == (k + 1) * (k + 2) // 2 - 1)
-
-        @pl.when(fresh)
-        def _():
-            load(k).wait()
-
         row = lax.broadcasted_iota(jnp.int32, (256, 1), 0)
         r_core = row // 128
         r_w = (row // ROWS) % 4
@@ -197,8 +196,21 @@
         blank = jnp.zeros((256, 4), jnp.float32)
         holes = jnp.concatenate([holes, blank, holes, blank], axis=1).astype(jnp.bfloat16)
         slab[p, :, :, :, V:] = holes.reshape(2, 4, ROWS, 128)
+        return carry
+
+    def compute(p):
+        q, j, k = pair_of(p)
+        is_a, u, w, off = place(p)
+        fresh = (p == 0) | (q == (k + 1) * (k + 2) // 2 - 1)
+
+        @pl.when(fresh)
+        def _():
+            load(k).wait()
+
+        source = (u + off) % 4
         cols = slab[p].reshape(2 * 4 * ROWS, 1024)
         wbuf[...] = lax.dot_general(vv[k], cols, NT_DIMS, preferred_element_type=jnp.float32)
+        holes = slab[p, :, :, :, V:].reshape(256, 128)
         variant = jnp.where(is_a, 0, 4) + source
         yc_row = yc_ref[pl.ds(variant, 1), :]
         lane = lax.broadcasted_iota(jnp.int32, (1, 128), 1)
@@ -253,29 +265,37 @@
             for turn in range(2):
                 second(s, turn).start()
 
+            @pl.when(s < EARLY)
+            def _():
+                second(s, 2).start()
+
         @pl.when((s >= LAG2) & (s < PAIRS + LAG2))
         def _():
             for turn in range(2):
                 second(s - LAG2, turn).wait_recv()
-            relay(s - LAG2).start()
+
+            @pl.when(s - LAG2 >= EARLY)
+            def _():
+                relay(s - LAG2).start()
 
         @pl.when((s >= LAG3) & (s < PAIRS + LAG3))
         def _():
             relay(s - LAG3).wait_recv()
             third(s - LAG3).start()
 
-        @pl.when(s == 1)
-        def _():
+        @pl.when(s == 0)
+        def _():
+            ints_in.wait()
             holes_in.wait()
             base_holes()
 
-        @pl.when((s >= 2) & (s < OW + 1))
-        def _():
-            turn_holes(s - 1)
-
-        @pl.when(s == OW + 1)
-        def _():
-            ints_in.wait()
+        @pl.when((s >= 1) & (s < OW))
+        def _():
+            turn_holes(s)
+
+        @pl.when(s < 5)
+        def _():
+            lax.fori_loop(3 * s, 3 * s + 3, prepare, 0)
 
         @pl.when(s >= LAG4)
         def _():
@@ -293,6 +313,9 @@
         def _():
             copy.wait_send()
 
+        return carry
+
+    def drain_rest(p, carry):
         for turn in range(2):
             second(p, turn).wait_send()
         relay(p).wait_send()
@@ -314,6 +337,7 @@
     for r in (1, 2, 3):
         to_group(r).start()
     ybox[y] = tile[...]
+    lax.fori_loop(0, PAIRS, drain_rest, 0)
     for r in (1, 2, 3):
         to_group(r).wait_recv()
     whole = ybox[0] + ybox[1] + ybox[2] + ybox[3]
@@ -350,7 +374,7 @@
     by_x = jnp.transpose(split, (0, 2, 1, 3)).reshape(4, 256)
     by_z = jnp.transpose(split, (1, 2, 0, 3)).reshape(4, 256)
     yc = jnp.concatenate([by_x, by_z], axis=0)
-    holes = jnp.pad(t2hole.reshape(OW, 60, 2 * V), ((0, 0), (0, 4), (0, 0)))
+    holes = t2hole.reshape(OW, 60, 2 * V)
     return yc, holes
 
 
@@ -371,7 +395,7 @@
             pltpu.VMEM((OW, 2 * V, 1024), jnp.bfloat16),
             pltpu.VMEM((2 * V, 256), jnp.float32),
             pltpu.VMEM((OW, 2 * V, 128), jnp.bfloat16),
-            pltpu.VMEM((OW, 64, 2 * V), jnp.bfloat16),
+            pltpu.VMEM((OW, 60, 2 * V), jnp.bfloat16),
             pltpu.VMEM((OW, OW, 60, V), jnp.bfloat16),
             pltpu.VMEM((2 * V, 128), jnp.float32),
             pltpu.SemaphoreType.DMA((2,)),

time: 81.6 us -> 79.8 us (0.978)
  Pallas kernels: 71.1 us -> 66.8 us
  other arithmetic: 0.69 us -> 2.14 us
  local copies, waits for them, and re-layouts: 8.2 us -> 9.21 us
    pallas_call x1, Pallas kernels: 71.1 us -> 66.8 us  [partial_energies(): pl.pallas_call(kernel, out_shape=[jax.ShapeDtypeStruct((8, 128), jnp.floa...]
    pad x1 -> x0, local copies, waits for them, and re-layouts: 1.09 us -> none  [tables(): holes = jnp.pad(t2hole.reshape(OW, 60, 2 * V), ((0, 0), (0, 4), (0, 0)))]
where the time goes in v3:
time: 79.8 us; the launch traced here: 79.5 us
  Pallas kernels  66.8 us (84%)
  local copies, waits for them, and re-layouts  9.21 us (12%)
  other arithmetic  2.14 us (3%)
  between operations  1.31 us (2%)
    pallas_call x1, Pallas kernels, partial_energies(): pl.pallas_call(kernel, out_shape=[jax.ShapeDtypeStruct((8, 128), jnp.floa...  66.8 us
    reshape x1, local copies, waits for them, and re-layouts, tables(): holes = t2hole.reshape(OW, 60, 2 * V)  3.73 us
    slice x2, local copies, waits for them, and re-layouts, shards(): return (trip[:slots, 0], orbital[:2, 0])  2.6 us

profile of v3, /device:TPU:1, one launch (start us, length us, event | category | flops | bytes accessed | tf_op | source)
XLA Modules:
  0.0 79.5 jit_solution(12819393143004902022)
XLA Ops:
  1.3 0.7 compare_select_fusion
  1.9 0.8 %add_bitcast_fusion = s32[6]{0:T(128)S(1)} fusion(s32[6,3]{0,1:T(4,128)} %param.10), kind=kLoop, calls=%fused_computation.13 | loop fusion | flops 120 | bytes 96 | tf_op jit(solution)/shard_map/eq | solution.py:436
  2.7 0.1 fusion
  2.8 0.6 pad.9.hit_ref
  3.4 1.3 %reshape.25.vir_ref = f32[1,896]{1,0:T(1,128)} reshape(f32[896]{0:T(1024)} %vsm_ref.1) | data formatting | bytes 7168 | tf_op jit(solution)/shard_map/reshape | solution.py:423
  4.7 0.8 reshape.26
  5.5 0.1 reshape.27
  5.6 0.1 reshape.28
  5.7 0.6 pad_maximum_fusion.yc_ref
  6.3 3.7 %reshape.24.hole_hbm = bf16[5,60,1792]{2,1,0:T(8,128)(2,1)} reshape(bf16[5,60,2,896]{3,2,1,0:T(2,128)(2,1)} %param.18) | data formatting | bytes 2150400 | tf_op jit(solution)/shard_map/reshape | solution.py:377
  10.1 66.8 %shard_map.113 = (f32[8,128]{1,0:T(8,128)}, f32[8,128]{1,0:T(8,128)}) custom-call(bf16[5,5,28,896]{3,2,1,0:T(8,128)(2,1)} %t2_ref.1, bf16[5,1792,896]{2,1,0:T(8,128)(2,1)} %bitcast.9, bf16[5,60,1792]{2,1,0:T(8,128)(2,1)} %reshape.24.hole_hbm, bf16[5,5,60,896]{3,2,1,0:T(8,128)(2,1)} %ih_hbm.1, f32[1,896]{1,0:T(1,128)} %reshape.25.vir_ref, ...), custom_call_target="tpu_custom_call" | custom-call | tf_op jit(solution)/shard_map/pallas_call | solution.py:385
  76.9 1.3 %slice_reduce_fusion = f32[6]{0:T(128)} fusion(f32[8,128]{1,0:T(8,128)} %get-tuple-element.4), kind=kLoop, calls=%fused_computation.3 | loop fusion | bytes 48 | tf_op jit(solution)/shard_map/slice | solution.py:441
  78.2 1.3 %slice_reduce_fusion.1 = f32[2]{0:T(128)} fusion(f32[8,128]{1,0:T(8,128)} %get-tuple-element.5), kind=kLoop, calls=%fused_computation.11 | loop fusion | bytes 16 | tf_op jit(solution)/shard_map/slice | solution.py:441
  (3 shorter events, 0.0 us)

commit v4 on v3

--- a/solution.py
+++ b/solution.py
@@ -10,10 +10,10 @@
 ROWS = 32
 PAIRS = 15
 OW = 5
-LEAD = 4
-LAG2 = 3
-LAG3 = 3
-LAG4 = 5
+LEAD = 15
+LAG2 = 4
+LAG3 = 4
+LAG4 = 6
 EARLY = 15
 CHUNK = 224
 NT_DIMS = (((1,), (1,)), ((), ()))
@@ -31,8 +31,8 @@
 
 
 def kernel(
-    t2_ref, vvvo_ref, hole_hbm, ih_hbm, vir_ref, yc_ref, hit_ref, occ_ref, vsm_ref, pick_ref,
-    trip_ref, orb_ref, src, slab, vv, wbuf, th_ref, hole_ref, ih_ref, xb_ref, isem, send1, recv1, send2, recv2, send3, recv3, vsem,
+    t2_ref, vvvo_ref, hole_hbm, ih_hbm, vir_ref, yc_ref, trips_ref, counts_ref, weights_ref, occ_ref, vsm_ref, pick_ref,
+    trip_ref, orb_ref, src, slab, vv, wbuf, th_ref, hole_ref, ih_ref, xb_ref, hit_ref, isem, send1, recv1, send2, recv2, send3, recv3, vsem,
     tile, ybox, part, vbox, ysend, yrecv, psend, precv,
 ):
     y = lax.axis_index("grp")
@@ -141,9 +141,16 @@
     for a in range(2):
         e_a = vsm_ref[pick_ref[a]]
         for c in range(V // 128):
-            lines = jnp.broadcast_to(vir_ref[:, c * 128:(c + 1) * 128], (128, 128))
+            lines = jnp.broadcast_to(vir_ref[c * 128:(c + 1) * 128][None, :], (128, 128))
             xb_ref[a * V + c * 128:a * V + (c + 1) * 128, :] = lines.T + e_a
     tile[...] = jnp.zeros_like(tile)
+    cells = lax.broadcasted_iota(jnp.int32, (1, 128), 1)
+    hit_ref[...] = jnp.zeros_like(hit_ref)
+    for n in range(6):
+        i, j, k = trips_ref[n, 0], trips_ref[n, 1], trips_ref[n, 2]
+        code = (k * (k + 1) // 2 + j) * OW + i
+        weight = jnp.where(n < counts_ref[0], weights_ref[n], 0).astype(jnp.float32)
+        hit_ref[n:n + 1, :] = jnp.where(cells == code, -weight, 0.0) / (V * V)
     tile[2:3, :] = jnp.sum(hit_ref[...], axis=0, keepdims=True)
     pl.semaphore_wait(barrier, 34)
 
@@ -156,23 +163,19 @@
 
     for p in range(LEAD):
         start_first(p)
-
-    def read_holes(i, at):
-        some = hole_ref[i, :, at:at + 128].astype(jnp.float32)
-        return jnp.concatenate([some, jnp.zeros((4, 128), jnp.float32)], axis=0)
 
     def turn_holes(i):
         for c in range(2 * V // 128):
             at = c * 128
-            base = read_holes(0, at)
-            this = read_holes(i, at)
+            base = hole_ref[0, :, at:at + 128].astype(jnp.float32)
+            this = hole_ref[i, :, at:at + 128].astype(jnp.float32)
             both = jnp.concatenate([base, -this], axis=0)
             th_ref[i, at:at + 128, :] = both.T.astype(jnp.bfloat16)
 
     def base_holes():
         for c in range(2 * V // 128):
             at = c * 128
-            base = read_holes(0, at)
+            base = hole_ref[0, :, at:at + 128].astype(jnp.float32)
             both = jnp.concatenate([-base, jnp.zeros_like(base)], axis=0)
             turned = both.T.astype(jnp.bfloat16)
             for k in range(OW):
@@ -345,7 +348,8 @@
     part[...] = mine
     vbox[vir] = mine
     orb = jnp.sum(whole[2:3, :] * whole, axis=1, keepdims=True)
-    orb_ref[...] = jnp.broadcast_to(orb, (8, 128))
+    for a in range(2):
+        orb_ref[a] = jnp.sum(orb[a:a + 1, :])
 
     def to_plane(r, carry):
         pltpu.make_async_remote_copy(
@@ -364,7 +368,8 @@
     others = vbox.at[pl.ds(0, 31)]
     pltpu.make_async_copy(others, others, precv).wait()
     trip = jnp.sum(jnp.sum(vbox[...], axis=0), axis=1, keepdims=True)
-    trip_ref[...] = jnp.broadcast_to(trip, (8, 128)) / 64
+    for n in range(6):
+        trip_ref[n] = jnp.sum(trip[n:n + 1, :] / 64)
     pltpu.make_async_copy(others, others, psend).wait()
 
 
@@ -374,30 +379,35 @@
     by_x = jnp.transpose(split, (0, 2, 1, 3)).reshape(4, 256)
     by_z = jnp.transpose(split, (1, 2, 0, 3)).reshape(4, 256)
     yc = jnp.concatenate([by_x, by_z], axis=0)
-    holes = t2hole.reshape(OW, 60, 2 * V)
+    holes = jnp.pad(t2hole.reshape(OW, 60, 2 * V), ((0, 0), (0, 4), (0, 0)))
     return yc, holes
 
 
-def partial_energies(t2pair, ints_vvvo, holes, ints_hole, vir_energy, yc, hit, occ_energy, a_pick):
+def partial_energies(
+    t2pair, ints_vvvo, holes, ints_hole, vir_energy, yc, triplets, counts, weights, occ_energy, a_pick
+):
     vmem = pl.BlockSpec(memory_space=pltpu.VMEM)
     smem = pl.BlockSpec(memory_space=pltpu.SMEM)
     hbm = pl.BlockSpec(memory_space=pl.ANY)
     return pl.pallas_call(
         kernel,
-        out_shape=[jax.ShapeDtypeStruct((8, 128), jnp.float32)] * 2,
+        out_shape=[
+            jax.ShapeDtypeStruct((6,), jnp.float32), jax.ShapeDtypeStruct((2,), jnp.float32),
+        ],
         in_specs=[
-            vmem, hbm, hbm, hbm, vmem, vmem, vmem, smem, smem, smem,
+            vmem, hbm, hbm, hbm, vmem, vmem, smem, smem, smem, smem, smem, smem,
         ],
-        out_specs=[vmem, vmem],
+        out_specs=[smem, smem],
         scratch_shapes=[
             pltpu.VMEM((PAIRS, ROWS, V), jnp.bfloat16),
             pltpu.VMEM((PAIRS, 2, 4, ROWS, 1024), jnp.bfloat16),
             pltpu.VMEM((OW, 2 * V, 1024), jnp.bfloat16),
             pltpu.VMEM((2 * V, 256), jnp.float32),
             pltpu.VMEM((OW, 2 * V, 128), jnp.bfloat16),
-            pltpu.VMEM((OW, 60, 2 * V), jnp.bfloat16),
+            pltpu.VMEM((OW, 64, 2 * V), jnp.bfloat16),
             pltpu.VMEM((OW, OW, 60, V), jnp.bfloat16),
             pltpu.VMEM((2 * V, 128), jnp.float32),
+            pltpu.VMEM((8, 128), jnp.float32),
             pltpu.SemaphoreType.DMA((2,)),
             pltpu.SemaphoreType.DMA((PAIRS,)),
             pltpu.SemaphoreType.DMA((PAIRS,)),
@@ -420,7 +430,7 @@
         ),
     )(
         t2pair, ints_vvvo.reshape(OW, 2 * V, V), holes, ints_hole,
-        vir_energy.reshape(1, V), yc, hit, occ_energy, vir_energy, a_pick,
+        vir_energy, yc, triplets, counts, weights, occ_energy, vir_energy, a_pick,
     )
 
 
@@ -429,16 +439,11 @@
 ):
     slots = triplets.shape[0]
     yc, holes = tables(vir_energy, t2hole)
-    code = (triplets[:, 2] * (triplets[:, 2] + 1) // 2 + triplets[:, 1]) * OW + triplets[:, 0]
-    live = jnp.arange(slots, dtype=jnp.int32) < counts[0]
-    factor = jnp.where(live, -weights.astype(jnp.float32) / (V * V), 0.0)
-    lanes = jnp.arange(128, dtype=jnp.int32)
-    hit = jnp.where(code[:, None] == lanes[None, :], factor[:, None], 0.0)
-    hit = jnp.pad(hit, ((0, 8 - slots), (0, 0)))
     trip, orbital = partial_energies(
-        t2pair, ints_vvvo, holes, ints_hole, vir_energy, yc, hit, occ_energy, a_pick
+        t2pair, ints_vvvo, holes, ints_hole, vir_energy, yc, triplets, counts, weights,
+        occ_energy, a_pick,
     )
-    return (trip[:slots, 0], orbital[:2, 0])
+    return (trip, orbital)
 
 
 def solution(mesh):

time: 79.8 us -> 75.9 us (0.951)
  local copies, waits for them, and re-layouts: 9.21 us -> 7.36 us
  other arithmetic: 2.14 us -> 0.61 us
    unnamed x0 -> x7, local copies, waits for them, and re-layouts: none -> 2.98 us
    slice x2 -> x0, local copies, waits for them, and re-layouts: 2.6 us -> none  [shards(): return (trip[:slots, 0], orbital[:2, 0])]
    reshape x2 -> x1, local copies, waits for them, and re-layouts: 5.01 us -> 2.99 us  [tables(): holes = jnp.pad(t2hole.reshape(OW, 60, 2 * V), ((0, 0), (0, 4), (0, 0)))]
    eq x1 -> x0, other arithmetic: 0.81 us -> none  [shards(): hit = jnp.where(code[:, None] == lanes[None, :], factor[:, None], 0.0)]
where the time goes in v4:
time: 75.9 us; the launch traced here: 75.7 us
  Pallas kernels  66.4 us (87%)
  local copies, waits for them, and re-layouts  7.36 us (10%)
  between operations  1.33 us (2%)
    pallas_call x1, Pallas kernels, partial_energies(): pl.pallas_call(kernel, out_shape=[jax.ShapeDtypeStruct((6,), jnp.float32)...  66.4 us
    reshape x1, local copies, waits for them, and re-layouts, tables(): holes = jnp.pad(t2hole.reshape(OW, 60, 2 * V), ((0, 0), (0, 4), (0, 0)))  2.99 us
    unnamed x7, local copies, waits for them, and re-layouts  2.98 us

profile of v4, /device:TPU:1, one launch (start us, length us, event | category | flops | bytes accessed | tf_op | source)
XLA Modules:
  0.0 75.7 jit_solution(16204711167013178884)
XLA Ops:
  0.6 3.0 %reshape.20 = bf16[5,60,1792]{2,1,0:T(8,128)(2,1)S(1)} reshape(bf16[5,60,2,896]{3,2,1,0:T(2,128)(2,1)} %param.18) | data formatting | bytes 2150400 | tf_op jit(solution)/shard_map/reshape | solution.py:382
  3.6 0.0 copy-start
  3.6 0.0 copy-start.1
  3.6 1.1 %pad.8.hole_hbm = bf16[5,64,1792]{2,1,0:T(8,128)(2,1)} pad(bf16[5,60,1792]{2,1,0:T(8,128)(2,1)S(1)} %reshape.20, bf16[]{:T(256)} %constant.1.clone.1), padding=0_0x0_4x0_0 | pad | bytes 2222082 | tf_op jit(solution)/shard_map/jit(_pad)/pad | solution.py:382
  4.7 0.0 copy-done
  4.7 0.1 reshape.21
  4.9 0.1 reshape.23
  5.0 0.1 reshape.22
  5.1 0.6 pad_maximum_fusion.yc_ref
  5.7 0.0 copy-done.1
  5.7 0.7 copy.16.trips_ref
  7.0 66.4 %shard_map.113 = (f32[6]{0:T(128)}, f32[2]{0:T(128)}) custom-call(bf16[5,5,28,896]{3,2,1,0:T(8,128)(2,1)} %t2_ref.1, bf16[5,1792,896]{2,1,0:T(8,128)(2,1)} %bitcast.5, bf16[5,64,1792]{2,1,0:T(8,128)(2,1)} %pad.8.hole_hbm, bf16[5,5,60,896]{3,2,1,0:T(8,128)(2,1)} %ih_hbm.1, f32[896]{0:T(1024)} %vsm_ref.1, f32[8,256]{1,0:T(8,128)} %pad_maximum_fusion.yc_ref, ...), custom_call_target="tpu_custom_call" | custom-call | tf_op jit(solution)/shard_map/pallas_call | solution.py:392
  73.4 1.1 %copy.20 = f32[6]{0:T(128)} copy(f32[6]{0:T(128)} %get-tuple-element.6) | data formatting | bytes 48
  74.5 1.2 %copy.21 = f32[2]{0:T(128)} copy(f32[2]{0:T(128)} %get-tuple-element.7) | data formatting | bytes 16
  (3 shorter events, 0.0 us)
Async XLA Ops:
  3.6 1.1 %copy-start = (f32[896]{0:T(1024)S(1)}, f32[896]{0:T(1024)}, u32[]{:S(2)}) copy-start(f32[896]{0:T(1024)} %vsm_ref.1) | copy-start | bytes 10756
  3.6 2.0 %copy-start.1 = (s32[6,3]{0,1:T(4,128)S(1)}, s32[6,3]{0,1:T(4,128)}, u32[]{:S(2)}) copy-start(s32[6,3]{0,1:T(4,128)} %param.10) | copy-start | bytes 220

commit v5 on v4

--- a/solution.py
+++ b/solution.py
@@ -164,22 +164,21 @@
     for p in range(LEAD):
         start_first(p)
 
-    def turn_holes(i):
-        for c in range(2 * V // 128):
-            at = c * 128
-            base = hole_ref[0, :, at:at + 128].astype(jnp.float32)
-            this = hole_ref[i, :, at:at + 128].astype(jnp.float32)
-            both = jnp.concatenate([base, -this], axis=0)
-            th_ref[i, at:at + 128, :] = both.T.astype(jnp.bfloat16)
-
-    def base_holes():
-        for c in range(2 * V // 128):
-            at = c * 128
-            base = hole_ref[0, :, at:at + 128].astype(jnp.float32)
-            both = jnp.concatenate([-base, jnp.zeros_like(base)], axis=0)
-            turned = both.T.astype(jnp.bfloat16)
-            for k in range(OW):
-                vv[k, at:at + 128, V:] = turned
+    def read_holes(i, a, at):
+        some = hole_ref[i, :, :, at:at + 128].astype(jnp.float32)[:, a, :]
+        return jnp.concatenate([some, jnp.zeros((4, 128), jnp.float32)], axis=0)
+
+    def turn_holes(c):
+        a, at = c // 7, (c % 7) * 128
+        row = c * 128
+        base = read_holes(0, a, at)
+        both = jnp.concatenate([-base, jnp.zeros_like(base)], axis=0)
+        turned = both.T.astype(jnp.bfloat16)
+        for k in range(OW):
+            vv[k, row:row + 128, V:] = turned
+        for i in range(1, OW):
+            both = jnp.concatenate([base, -read_holes(i, a, at)], axis=0)
+            th_ref[i, row:row + 128, :] = both.T.astype(jnp.bfloat16)
 
     def prepare(p, carry):
         q, j, k = pair_of(p)
@@ -290,11 +289,12 @@
         def _():
             ints_in.wait()
             holes_in.wait()
-            base_holes()
-
-        @pl.when((s >= 1) & (s < OW))
-        def _():
-            turn_holes(s)
+
+        for part_at in range(5):
+            @pl.when(s == part_at)
+            def _():
+                for c in range(3 * part_at, min(14, 3 * part_at + 3)):
+                    turn_holes(c)
 
         @pl.when(s < 5)
         def _():
@@ -373,14 +373,13 @@
     pltpu.make_async_copy(others, others, psend).wait()
 
 
-def tables(vir_energy, t2hole):
+def tables(vir_energy):
     split = vir_energy.reshape(4, 4, 2, BLOCK)
     split = jnp.pad(split, ((0, 0), (0, 0), (0, 0), (0, ROWS - BLOCK)), constant_values=1.0)
     by_x = jnp.transpose(split, (0, 2, 1, 3)).reshape(4, 256)
     by_z = jnp.transpose(split, (1, 2, 0, 3)).reshape(4, 256)
     yc = jnp.concatenate([by_x, by_z], axis=0)
-    holes = jnp.pad(t2hole.reshape(OW, 60, 2 * V), ((0, 0), (0, 4), (0, 0)))
-    return yc, holes
+    return yc
 
 
 def partial_energies(
@@ -404,7 +403,7 @@
             pltpu.VMEM((OW, 2 * V, 1024), jnp.bfloat16),
             pltpu.VMEM((2 * V, 256), jnp.float32),
             pltpu.VMEM((OW, 2 * V, 128), jnp.bfloat16),
-            pltpu.VMEM((OW, 64, 2 * V), jnp.bfloat16),
+            pltpu.VMEM((OW, 60, 2, V), jnp.bfloat16),
             pltpu.VMEM((OW, OW, 60, V), jnp.bfloat16),
             pltpu.VMEM((2 * V, 128), jnp.float32),
             pltpu.VMEM((8, 128), jnp.float32),
@@ -438,9 +437,9 @@
     triplets, counts, weights, a_pick, occ_energy, vir_energy, ints_vvvo, t2pair, t2hole, ints_hole
 ):
     slots = triplets.shape[0]
-    yc, holes = tables(vir_energy, t2hole)
+    yc = tables(vir_energy)
     trip, orbital = partial_energies(
-        t2pair, ints_vvvo, holes, ints_hole, vir_energy, yc, triplets, counts, weights,
+        t2pair, ints_vvvo, t2hole, ints_hole, vir_energy, yc, triplets, counts, weights,
         occ_energy, a_pick,
     )
     return (trip, orbital)

time: 75.9 us -> 74.7 us (0.984)
  local copies, waits for them, and re-layouts: 7.36 us -> 4.61 us
  Pallas kernels: 66.4 us -> 68 us
    reshape x1 -> x0, local copies, waits for them, and re-layouts: 2.99 us -> none  [tables(): holes = jnp.pad(t2hole.reshape(OW, 60, 2 * V), ((0, 0), (0, 4), (0, 0)))]
    pallas_call x1, Pallas kernels: 66.4 us -> 68 us  [partial_energies(): pl.pallas_call(kernel, out_shape=[jax.ShapeDtypeStruct((6,), jnp.float32)...]
    pad x1 -> x0, local copies, waits for them, and re-layouts: 1.08 us -> none  [tables(): holes = jnp.pad(t2hole.reshape(OW, 60, 2 * V), ((0, 0), (0, 4), (0, 0)))]
    unnamed x7 -> x3, local copies, waits for them, and re-layouts: 2.98 us -> 3.62 us
where the time goes in v5:
time: 74.7 us; the launch traced here: 74.5 us
  Pallas kernels  68 us (91%)
  local copies, waits for them, and re-layouts  4.61 us (6%)
  between operations  1.31 us (2%)
    pallas_call x1, Pallas kernels, partial_energies(): pl.pallas_call(kernel, out_shape=[jax.ShapeDtypeStruct((6,), jnp.float32)...  68 us
    unnamed x3, local copies, waits for them, and re-layouts  3.62 us

profile of v5, /device:TPU:1, one launch (start us, length us, event | category | flops | bytes accessed | tf_op | source)
XLA Modules:
  0.0 74.5 jit_solution(17817277192490547872)
XLA Ops:
  0.6 0.8 %reshape.17 = f32[4,4,2,28]{3,2,1,0:T(2,128)S(1)} reshape(f32[896]{0:T(1024)} %vsm_ref.1) | data formatting | bytes 7168 | tf_op jit(solution)/shard_map/reshape | solution.py:377
  1.5 0.1 reshape.18
  1.6 0.1 reshape.19
  1.7 0.6 pad_maximum_fusion.yc_ref
  2.3 1.4 %copy.16.trips_ref = s32[6,3]{1,0:T(8,128)} copy(s32[6,3]{0,1:T(4,128)} %param.10) | data formatting | bytes 144 | tf_op args[0]
  4.3 68.0 %shard_map.113 = (f32[6]{0:T(128)}, f32[2]{0:T(128)}) custom-call(bf16[5,5,28,896]{3,2,1,0:T(8,128)(2,1)} %t2_ref.1, bf16[5,1792,896]{2,1,0:T(8,128)(2,1)} %bitcast.5, bf16[5,60,2,896]{3,2,1,0:T(2,128)(2,1)} %hole_hbm.1, bf16[5,5,60,896]{3,2,1,0:T(8,128)(2,1)} %ih_hbm.1, f32[896]{0:T(1024)} %vsm_ref.1, f32[8,256]{1,0:T(8,128)} %pad_maximum_fusion.yc_ref, ...), custom_call_target="tpu_custom_call" | custom-call | tf_op jit(solution)/shard_map/pallas_call | solution.py:391
  72.3 1.1 %copy.20 = f32[6]{0:T(128)} copy(f32[6]{0:T(128)} %get-tuple-element.6) | data formatting | bytes 48
  73.4 1.1 %copy.21 = f32[2]{0:T(128)} copy(f32[2]{0:T(128)} %get-tuple-element.7) | data formatting | bytes 16
  (3 shorter events, 0.0 us)
